TPU v7x, 256 devices: a whole 4x4x8 slice. The times are simulated.
256 devices in a mesh: gx: 8 (over x, core), gy: 4 (over y), gz: 8 (over z).
Axes of the slice: x: 4, y: 4, z: 8, core: 2. Of those that a mesh axis runs over, the one named last changes fastest.
Arguments:
- dual_rhs: float32 [8, 4, 8, 3, 300, 128], P('gx', 'gy', 'gz'), may hold values from -6 to 6
- local_flex: bfloat16 [8, 4, 8, 1800, 1800], P('gx', 'gy', 'gz'), as said below
- corner_coupling: bfloat16 [8, 4, 8, 24, 1800], P('gx', 'gy', 'gz'), may hold values from -0.375 to 0.375
- face_stiffness: bfloat16 [8, 4, 8, 6, 300, 300], P('gx', 'gy', 'gz'), as said below
- coarse_inverse: bfloat16 [441, 441], replicated, as said below
- corner_ids: int32 [8, 4, 8, 8], P('gx', 'gy', 'gz'), may hold values from -1 to 146, as said below
Outputs:
- multipliers: float32 [8, 4, 8, 3, 300, 128], P('gx', 'gy', 'gz')
- residual: float32 [8, 4, 8, 3, 300, 128], P('gx', 'gy', 'gz')
Inputs may be any that keep to these rules, and one draw needn't show every extreme that they name: `local_flex`: each subdomain's matrix is symmetric positive definite. `face_stiffness`: each face block is symmetric positive definite. `coarse_inverse`: symmetric positive definite. `corner_ids`: entry k = 4 kx + 2 ky + kz of subdomain (i, j, l) is the number of the corner at lattice point (i + kx, j + ky, l + kz) when that point has all coordinates strictly between 0 and the subdomain counts, else -1; the 147 interior corners are numbered by a permutation, so subdomains sharing a corner name the same node.
All inputs are finite; a program needn't handle non-finite values.
Results may differ from a plain program's by a relative error of at most 0.04.
Values may be sent and summed in bfloat16 or wider, within the bound.
No kernel may reach another device: no remote copies, remote signals or barrier semaphores. Data moves between devices by JAX's collectives and lax.ppermute only.
A program may use at most 64 MiB of HBM per device.

v0:
```python
import jax
import jax.numpy as jnp
from jax import lax
from jax.sharding import Mesh
from jax.sharding import PartitionSpec as P

ITERS = 3
GX = ("gx_0", "gx_1")


def with_halo(value, sides, width):
    for axis, dim in sides:
        size, length = (lax.axis_size(axis), value.shape[dim])
        up = [(i, (i + 1) % size) for i in range(size - 1)]
        down = [(j, i) for i, j in up]
        last = lax.slice_in_dim(value, length - width, length, axis=dim)
        first = lax.slice_in_dim(value, 0, width, axis=dim)
        before = lax.ppermute(last, axis, up)
        after = lax.ppermute(first, axis, down)
        value = jnp.concatenate([before, value, after], axis=dim)
    return value


def from_everyone(value, axis):
    copies = jnp.broadcast_to(value, (lax.axis_size(axis), *value.shape))
    return lax.all_to_all(copies, axis, split_axis=0, concat_axis=0, tiled=True)


def of_everyone(value, axis):
    return from_everyone(value, axis).sum(axis=0)


def over_axes(value, axes):
    far, near = axes
    nearer = of_everyone(value, near)
    return of_everyone(nearer, far)


def in_blocks(value, dim, size):
    lengths = value.shape
    pieces = value.reshape(*lengths[:dim], size, lengths[dim] // size, *lengths[dim + 1 :])
    return jnp.moveaxis(pieces, dim, 0)


def sum_at_owner(value, axis, dim):
    pieces = in_blocks(value, dim, lax.axis_size(axis))
    arrived = lax.all_to_all(pieces, axis, split_axis=0, concat_axis=0, tiled=True)
    return arrived.astype(jnp.float32).sum(axis=0)


def summed_rows(value, axes, dim):
    far, near = axes
    pieces = in_blocks(value, dim, lax.axis_size(far))
    nearer = sum_at_owner(pieces, near, dim + 1)
    arrived = lax.all_to_all(
        nearer.astype(jnp.bfloat16), far, split_axis=0, concat_axis=0, tiled=True
    )
    return arrived.astype(jnp.float32).sum(axis=0)


def filled_up(lines, size):
    spare = -len(lines) % size
    return jnp.pad(lines, [(0, spare)] + [(0, 0)] * (lines.ndim - 1))


def in_order(pieces, dim):
    lengths = list(pieces.shape[1:])
    lengths[dim] *= pieces.shape[0]
    return jnp.moveaxis(pieces, 0, dim).reshape(lengths)


def whole_of(value, axes, dim):
    far, near = axes
    first = from_everyone(value, far)
    pieces = jnp.swapaxes(from_everyone(first, near), 0, 1)
    return in_order(pieces.reshape(-1, *value.shape), dim)


def sum_by_parts(value, axes):
    lines = value.reshape(-1)
    own = summed_rows(filled_up(lines, lax.axis_size(axes[0]) * lax.axis_size(axes[1])), axes, 0)
    whole = whole_of(own.astype(jnp.bfloat16), axes, 0)
    return whole[: len(lines)].reshape(value.shape).astype(jnp.float32)


def face_neighbours(face_pairs):
    along_x = with_halo(face_pairs[0].astype(jnp.bfloat16), ((GX, 0),), 1).astype(jnp.float32)
    along_y = with_halo(face_pairs[1].astype(jnp.bfloat16), (("gy", 0),), 1).astype(jnp.float32)
    along_z = with_halo(face_pairs[2].astype(jnp.bfloat16), (("gz", 0),), 1).astype(jnp.float32)
    return [along_x, along_y, along_z]


def face_jump(values, face_mask):
    extended = face_neighbours([values[0:2], values[2:4], values[4:6]])
    face_list = []
    for bordered in extended:
        face_list.append(bordered[0] - bordered[1])
        face_list.append(bordered[2] - bordered[3])
    return jnp.stack(face_list) * face_mask[:, None, None]


def duplicate(owned, face_mask):
    empty = jnp.zeros_like(owned[0])
    extended = face_neighbours([jnp.stack([empty, owned[axis_pos]]) for axis_pos in range(3)])
    face_list = []
    for axis_pos in range(3):
        face_list.append(extended[axis_pos][0])
        face_list.append(owned[axis_pos])
    return jnp.stack(face_list) * face_mask[:, None, None]


def neighbour_stiffness(stiffness):
    along_x = with_halo(stiffness[0:2], ((GX, 0),), 1)
    along_y = with_halo(stiffness[2:4], (("gy", 0),), 1)
    along_z = with_halo(stiffness[4:6], (("gz", 0),), 1)
    return jnp.stack([along_x[0], along_x[3], along_y[0], along_y[3], along_z[0], along_z[3]])


def owned_inner(left, right):
    return jnp.sum(left[1::2] * right[1::2], axis=(0, 1))


def global_sum(local_value):
    return over_axes(local_value, (("gx_0", "gx_1"), ("gy", "gz")))


def body(dual_rhs, local_flex, corner_coupling, face_stiffness, coarse_inverse, corner_ids):
    owned_rhs = dual_rhs[0, 0, 0]
    flex = local_flex[0, 0, 0]
    coupling = corner_coupling[0, 0, 0]
    stiffness = face_stiffness[0, 0, 0]
    corner_list = corner_ids[0, 0, 0]
    face_count, face_width, columns = (stiffness.shape[0], stiffness.shape[1], owned_rhs.shape[2])
    coarse_rows = coarse_inverse.shape[0]
    face_sign = jnp.array([-1.0, 1.0, -1.0, 1.0, -1.0, 1.0], jnp.float32)[:, None, None]
    place_x = lax.axis_index(GX)
    place_y = lax.axis_index("gy")
    place_z = lax.axis_index("gz")
    face_mask = jnp.stack(
        [
            place_x > 0,
            place_x < lax.axis_size(GX) - 1,
            place_y > 0,
            place_y < lax.axis_size("gy") - 1,
            place_z > 0,
            place_z < lax.axis_size("gz") - 1,
        ]
    ).astype(jnp.float32)
    coupling_wide = coupling.astype(jnp.float32)
    dof_ids = jnp.where(
        corner_list[:, None] >= 0,
        3 * corner_list[:, None] + jnp.arange(3, dtype=jnp.int32)[None, :],
        -1,
    ).reshape(-1)
    assembly = (jnp.arange(coarse_rows, dtype=jnp.int32)[:, None] == dof_ids[None, :]).astype(
        jnp.float32
    )
    beyond = neighbour_stiffness(stiffness)

    def precondition(dual):
        halved = (0.5 * face_sign * dual).astype(jnp.bfloat16)
        own_part = jnp.einsum("fij,fjr->fir", stiffness, halved, preferred_element_type=jnp.float32)
        far_part = jnp.einsum("fij,fjr->fir", beyond, halved, preferred_element_type=jnp.float32)
        return 0.5 * face_sign * (own_part + far_part) * face_mask[:, None, None]

    residual = duplicate(owned_rhs, face_mask)
    multiplier = jnp.zeros_like(residual)
    precond_res = precondition(residual)
    rho_now = global_sum(owned_inner(residual, precond_res))
    direction = precond_res
    for iteration in range(ITERS):
        signed = (
            (face_sign * direction).astype(jnp.bfloat16).reshape(face_count * face_width, columns)
        )
        local_local_image = jnp.dot(flex, signed, preferred_element_type=jnp.float32)
        corner_part = jnp.dot(coupling, signed, preferred_element_type=jnp.float32)
        coarse_part = jnp.dot(assembly, corner_part, precision=lax.Precision.HIGHEST)
        dual_coarse_rhs = sum_by_parts(
            coarse_part.astype(jnp.bfloat16), (("gx_0", "gx_1"), ("gy", "gz"))
        )
        coarse_sol = jnp.dot(
            coarse_inverse, dual_coarse_rhs.astype(jnp.bfloat16), preferred_element_type=jnp.float32
        )
        corner_sol = lax.dot_general(
            assembly, coarse_sol, (((0,), (0,)), ((), ())), precision=lax.Precision.HIGHEST
        )
        displaced = local_local_image + lax.dot_general(
            coupling_wide, corner_sol, (((0,), (0,)), ((), ())), precision=lax.Precision.HIGHEST
        )
        curvature = global_sum(jnp.sum(signed.astype(jnp.float32) * displaced, axis=0))
        image = face_jump(displaced.reshape(face_count, face_width, columns), face_mask)
        image, curvature = (image, curvature)
        step_size = rho_now / curvature
        multiplier = multiplier + step_size * direction
        residual = residual - step_size * image
        if iteration + 1 < ITERS:
            precond_res = precondition(residual)
            rho_next = global_sum(owned_inner(residual, precond_res))
            direction = precond_res + rho_next / rho_now * direction
            rho_now = rho_next
    return (multiplier[1::2][None, None, None], residual[1::2][None, None, None])


def solution(mesh):
    torus = Mesh(
        mesh.devices.reshape(4, 2, mesh.shape["gy"], mesh.shape["gz"]), ("gx_0", "gx_1", "gy", "gz")
    )
    in_specs = (
        P(GX, "gy", "gz", None, None, None),
        P(GX, "gy", "gz", None, None),
        P(GX, "gy", "gz", None, None),
        P(GX, "gy", "gz", None, None, None),
        P(),
        P(GX, "gy", "gz", None),
    )
    out_specs = (P(GX, "gy", "gz", None, None, None), P(GX, "gy", "gz", None, None, None))
    return jax.shard_map(body, mesh=torus, in_specs=in_specs, out_specs=out_specs, check_vma=False)
```

profile of v0, /device:TPU:1, one launch (start us, length us, event | category | flops | bytes accessed | tf_op | source)
XLA Modules:
  0.0 401.6 jit_solution(9360596173612316954)
XLA Ops:
  36.2 6.8 %collective-permute-done.8 = bf16[1,300,300]{2,1,0:T(8,128)(2,1)S(1)} collective-permute-done((bf16[1,300,300]{2,1,0:T(8,128)(2,1)S(1)}, bf16[1,300,300]{2,1,0:T(8,128)(2,1)S(1)}, u32[]{:S(2)}, u32[]{:S(2)}) %collective-permute-start.8) | collective-permute-done | bytes 180032 | tf_op jit(solution)/shard_map/ppermute | solution.py:19
  48.5 19.0 %all_to_all.156 = bf16[32,8,221]{2,1,0:T(8,128)(2,1)S(1)} all-to-all(bf16[32,8,221]{2,1,0:T(8,128)(2,1)S(1)} %copy.60), channel_id=1, replica_groups=mesh['gx_0'=4,'gx_1'=2,'gy'=4,'gz'=8] {'gy','gz'}, dimensions={0} | all-to-all | bytes 226304 | tf_op jit(solution)/shard_map/all_to_all | solution.py:47
  68.1 6.5 %all-to-all-start.3 = ((bf16[8,1,221]{2,1,0:T(2,128)(2,1)}), bf16[8,1,221]{2,1,0:T(2,128)(2,1)S(1)}, u32[]{:S(2)}, u32[]{:S(2)}) async-start(bf16[8,1,221]{2,1,0:T(2,128)(2,1)} %copy.61), calls=%async_computation.3 | async-start | bytes 16384 | tf_op jit(solution)/shard_map/all_to_all | solution.py:55
  83.7 8.6 %all-to-all-done = f32[32,1,128]{2,1,0:T(1,128)S(1)} async-done(((f32[32,1,128]{2,1,0:T(1,128)}), f32[32,1,128]{2,1,0:T(1,128)S(1)}, u32[]{:S(2)}, u32[]{:S(2)}) %all-to-all-start) | async-done | bytes 16416 | tf_op jit(solution)/shard_map/all_to_all | solution.py:26
  92.9 5.1 %all-to-all-start.4 = ((bf16[8,1,221]{2,1,0:T(2,128)(2,1)}), bf16[8,1,221]{2,1,0:T(2,128)(2,1)S(1)}, u32[]{:S(2)}, u32[]{:S(2)}) async-start(bf16[8,1,221]{2,1,0:T(2,128)(2,1)} %broadcast_in_dim.94), calls=%async_computation.4 | async-start | bytes 16384 | tf_op jit(solution)/shard_map/all_to_all | solution.py:26
  116.2 6.0 %fusion.4 = f32[128,1800]{0,1:T(8,128)} fusion(bf16[1800,128]{1,0:T(8,128)(2,1)S(1)} %reshape.266, bf16[1,1,1,1800,1800]{4,3,2,1,0:T(8,128)(2,1)} %param.8), kind=kOutput, calls=%fused_computation.4 | convolution fusion | flops 829440000 | bytes 7862400 | tf_op jit(solution)/shard_map/dot_general | solution.py:175
  128.5 6.1 %all-to-all-start.6 = ((f32[32,1,128]{2,1,0:T(1,128)}), f32[32,1,128]{2,1,0:T(1,128)S(1)}, u32[]{:S(2)}, u32[]{:S(2)}) async-start(f32[32,1,128]{2,1,0:T(1,128)} %broadcast_in_dim.96), calls=%async_computation.6 | async-start | bytes 32768 | tf_op jit(solution)/shard_map/all_to_all | solution.py:26
  143.8 5.6 %all-to-all-start.7 = ((f32[8,1,128]{2,1,0:T(1,128)}), f32[8,1,128]{2,1,0:T(1,128)S(1)}, u32[]{:S(2)}, u32[]{:S(2)}) async-start(f32[8,1,128]{2,1,0:T(1,128)} %broadcast_in_dim.97), calls=%async_computation.7 | async-start | bytes 8192 | tf_op jit(solution)/shard_map/all_to_all | solution.py:26
  164.6 15.1 %all_to_all.157 = f32[32,1,128]{2,1,0:T(1,128)S(1)} all-to-all(f32[32,1,128]{2,1,0:T(1,128)S(1)} %broadcast_in_dim.98), channel_id=1, replica_groups=mesh['gx_0'=4,'gx_1'=2,'gy'=4,'gz'=8] {'gy','gz'}, dimensions={0} | all-to-all | bytes 32768 | tf_op jit(solution)/shard_map/all_to_all | solution.py:26
  179.7 12.6 %all_to_all.158 = f32[8,1,128]{2,1,0:T(1,128)S(1)} all-to-all(f32[8,1,128]{2,1,0:T(1,128)S(1)} %broadcast_in_dim.99), channel_id=1, replica_groups=mesh['gx_0'=4,'gx_1'=2,'gy'=4,'gz'=8] {'gx_0','gx_1'}, dimensions={0} | all-to-all | bytes 8192 | tf_op jit(solution)/shard_map/all_to_all | solution.py:26
  198.1 12.1 %all_to_all.159 = bf16[32,8,221]{2,1,0:T(8,128)(2,1)S(1)} all-to-all(bf16[32,8,221]{2,1,0:T(8,128)(2,1)S(1)} %copy.67), channel_id=1, replica_groups=mesh['gx_0'=4,'gx_1'=2,'gy'=4,'gz'=8] {'gy','gz'}, dimensions={0} | all-to-all | bytes 226304 | tf_op jit(solution)/shard_map/all_to_all | solution.py:47
  210.3 9.1 %all_to_all.160 = bf16[8,1,221]{2,1,0:T(2,128)(2,1)S(1)} all-to-all(bf16[8,1,221]{2,1,0:T(2,128)(2,1)S(1)} %copy.68), channel_id=1, replica_groups=mesh['gx_0'=4,'gx_1'=2,'gy'=4,'gz'=8] {'gx_0','gx_1'}, dimensions={0} | all-to-all | bytes 7072 | tf_op jit(solution)/shard_map/all_to_all | solution.py:55
  219.4 7.7 %all_to_all.161 = bf16[8,1,221]{2,1,0:T(2,128)(2,1)S(1)} all-to-all(bf16[8,1,221]{2,1,0:T(2,128)(2,1)S(1)} %broadcast_in_dim.100), channel_id=1, replica_groups=mesh['gx_0'=4,'gx_1'=2,'gy'=4,'gz'=8] {'gx_0','gx_1'}, dimensions={0} | all-to-all | bytes 7072 | tf_op jit(solution)/shard_map/all_to_all | solution.py:26
  231.6 6.0 %fusion.2 = f32[128,1800]{0,1:T(8,128)} fusion(bf16[1800,128]{1,0:T(8,128)(2,1)S(1)} %reshape.268, bf16[1,1,1,1800,1800]{4,3,2,1,0:T(8,128)(2,1)} %param.8), kind=kOutput, calls=%fused_computation.2 | convolution fusion | flops 829440000 | bytes 7862400 | tf_op jit(solution)/shard_map/dot_general | solution.py:175
  246.3 6.1 %all-to-all-start.14 = ((f32[32,1,128]{2,1,0:T(1,128)}), f32[32,1,128]{2,1,0:T(1,128)S(1)}, u32[]{:S(2)}, u32[]{:S(2)}) async-start(f32[32,1,128]{2,1,0:T(1,128)} %broadcast_in_dim.102), calls=%async_computation.14 | async-start | bytes 32768 | tf_op jit(solution)/shard_map/all_to_all | solution.py:26
  261.6 5.6 %all-to-all-start.15 = ((f32[8,1,128]{2,1,0:T(1,128)}), f32[8,1,128]{2,1,0:T(1,128)S(1)}, u32[]{:S(2)}, u32[]{:S(2)}) async-start(f32[8,1,128]{2,1,0:T(1,128)} %broadcast_in_dim.103), calls=%async_computation.15 | async-start | bytes 8192 | tf_op jit(solution)/shard_map/all_to_all | solution.py:26
  288.1 16.0 %all_to_all.162 = f32[32,1,128]{2,1,0:T(1,128)S(1)} all-to-all(f32[32,1,128]{2,1,0:T(1,128)S(1)} %broadcast_in_dim.104), channel_id=1, replica_groups=mesh['gx_0'=4,'gx_1'=2,'gy'=4,'gz'=8] {'gy','gz'}, dimensions={0} | all-to-all | bytes 32768 | tf_op jit(solution)/shard_map/all_to_all | solution.py:26
  304.1 12.6 %all_to_all.163 = f32[8,1,128]{2,1,0:T(1,128)S(1)} all-to-all(f32[8,1,128]{2,1,0:T(1,128)S(1)} %broadcast_in_dim.105), channel_id=1, replica_groups=mesh['gx_0'=4,'gx_1'=2,'gy'=4,'gz'=8] {'gx_0','gx_1'}, dimensions={0} | all-to-all | bytes 8192 | tf_op jit(solution)/shard_map/all_to_all | solution.py:26
  319.2 12.1 %all_to_all.164 = bf16[32,8,221]{2,1,0:T(8,128)(2,1)S(1)} all-to-all(bf16[32,8,221]{2,1,0:T(8,128)(2,1)S(1)} %copy.74), channel_id=1, replica_groups=mesh['gx_0'=4,'gx_1'=2,'gy'=4,'gz'=8] {'gy','gz'}, dimensions={0} | all-to-all | bytes 226304 | tf_op jit(solution)/shard_map/all_to_all | solution.py:47
  331.4 9.1 %all_to_all.165 = bf16[8,1,221]{2,1,0:T(2,128)(2,1)S(1)} all-to-all(bf16[8,1,221]{2,1,0:T(2,128)(2,1)S(1)} %copy.75), channel_id=1, replica_groups=mesh['gx_0'=4,'gx_1'=2,'gy'=4,'gz'=8] {'gx_0','gx_1'}, dimensions={0} | all-to-all | bytes 7072 | tf_op jit(solution)/shard_map/all_to_all | solution.py:55
  340.5 7.7 %all_to_all.166 = bf16[8,1,221]{2,1,0:T(2,128)(2,1)S(1)} all-to-all(bf16[8,1,221]{2,1,0:T(2,128)(2,1)S(1)} %broadcast_in_dim.106), channel_id=1, replica_groups=mesh['gx_0'=4,'gx_1'=2,'gy'=4,'gz'=8] {'gx_0','gx_1'}, dimensions={0} | all-to-all | bytes 7072 | tf_op jit(solution)/shard_map/all_to_all | solution.py:26
  352.7 6.0 %fusion = f32[128,1800]{0,1:T(8,128)} fusion(bf16[1800,128]{1,0:T(8,128)(2,1)S(1)} %reshape.270, bf16[1,1,1,1800,1800]{4,3,2,1,0:T(8,128)(2,1)} %param.8), kind=kOutput, calls=%fused_computation | convolution fusion | flops 829440000 | bytes 7862400 | tf_op jit(solution)/shard_map/dot_general | solution.py:175
  365.0 6.1 %all-to-all-start.22 = ((f32[32,1,128]{2,1,0:T(1,128)}), f32[32,1,128]{2,1,0:T(1,128)S(1)}, u32[]{:S(2)}, u32[]{:S(2)}) async-start(f32[32,1,128]{2,1,0:T(1,128)} %broadcast_in_dim.108), calls=%async_computation.22 | async-start | bytes 32768 | tf_op jit(solution)/shard_map/all_to_all | solution.py:26
  380.3 5.6 %all-to-all-start.23 = ((f32[8,1,128]{2,1,0:T(1,128)}), f32[8,1,128]{2,1,0:T(1,128)S(1)}, u32[]{:S(2)}, u32[]{:S(2)}) async-start(f32[8,1,128]{2,1,0:T(1,128)} %broadcast_in_dim.109), calls=%async_computation.23 | async-start | bytes 8192 | tf_op jit(solution)/shard_map/all_to_all | solution.py:26
  (281 shorter events, 186.6 us)
Async XLA Ops:
  2.5 19.5 %collective-permute-start = (bf16[1,300,128]{2,1,0:T(8,128)(2,1)}, bf16[1,300,128]{2,1,0:T(8,128)(2,1)}, u32[]{:S(2)}, u32[]{:S(2)}) collective-permute-start(bf16[1,300,128]{2,1,0:T(8,128)(2,1)} %bitcast.185), channel_id=1, source_target_pairs={{0,32},{32,64},{64,96},{96,128},{128,160},{160,192},{192,224},{1,3... | collective-permute-start | bytes 230408 | tf_op jit(solution)/shard_map/ppermute | solution.py:18
  7.6 17.9 %collective-permute-start.1 = (bf16[1,300,128]{2,1,0:T(8,128)(2,1)}, bf16[1,300,128]{2,1,0:T(8,128)(2,1)}, u32[]{:S(2)}, u32[]{:S(2)}) collective-permute-start(bf16[1,300,128]{2,1,0:T(8,128)(2,1)} %bitcast.186), channel_id=1, source_target_pairs={{0,8},{8,16},{16,24},{1,9},{9,17},{17,25},{2,10},{10,18},{18,26},{... | collective-permute-start | bytes 230408 | tf_op jit(solution)/shard_map/ppermute | solution.py:18
  12.1 15.7 %collective-permute-start.2 = (bf16[1,300,128]{2,1,0:T(8,128)(2,1)}, bf16[1,300,128]{2,1,0:T(8,128)(2,1)}, u32[]{:S(2)}, u32[]{:S(2)}) collective-permute-start(bf16[1,300,128]{2,1,0:T(8,128)(2,1)} %bitcast.187), channel_id=1, source_target_pairs={{0,1},{1,2},{2,3},{3,4},{4,5},{5,6},{6,7},{8,9},{9,10},{10,11},{11... | collective-permute-start | bytes 230408 | tf_op jit(solution)/shard_map/ppermute | solution.py:18
  17.3 16.1 %collective-permute-start.3 = (bf16[1,300,300]{2,1,0:T(8,128)(2,1)}, bf16[1,300,300]{2,1,0:T(8,128)(2,1)S(1)}, u32[]{:S(2)}, u32[]{:S(2)}) collective-permute-start(bf16[1,300,300]{2,1,0:T(8,128)(2,1)} %get-tuple-element.18), channel_id=1, source_target_pairs={{0,32},{32,64},{64,96},{96,128},{128,160},{160,192},{192,224},{1,3... | collective-permute-start | bytes 540008 | tf_op jit(solution)/shard_map/ppermute | solution.py:18
  19.8 14.9 %collective-permute-start.4 = (bf16[1,300,300]{2,1,0:T(8,128)(2,1)}, bf16[1,300,300]{2,1,0:T(8,128)(2,1)S(1)}, u32[]{:S(2)}, u32[]{:S(2)}) collective-permute-start(bf16[1,300,300]{2,1,0:T(8,128)(2,1)} %get-tuple-element.17), channel_id=1, source_target_pairs={{32,0},{64,32},{96,64},{128,96},{160,128},{192,160},{224,192},{33,... | collective-permute-start | bytes 540008 | tf_op jit(solution)/shard_map/ppermute | solution.py:19
  22.0 12.8 %collective-permute-start.5 = (bf16[1,300,300]{2,1,0:T(8,128)(2,1)}, bf16[1,300,300]{2,1,0:T(8,128)(2,1)S(1)}, u32[]{:S(2)}, u32[]{:S(2)}) collective-permute-start(bf16[1,300,300]{2,1,0:T(8,128)(2,1)} %get-tuple-element.16), channel_id=1, source_target_pairs={{0,8},{8,16},{16,24},{1,9},{9,17},{17,25},{2,10},{10,18},{18,26},{... | collective-permute-start | bytes 540008 | tf_op jit(solution)/shard_map/ppermute | solution.py:18
  79.8 12.4 %all-to-all-start = ((f32[32,1,128]{2,1,0:T(1,128)}), f32[32,1,128]{2,1,0:T(1,128)S(1)}, u32[]{:S(2)}, u32[]{:S(2)}) async-start(f32[32,1,128]{2,1,0:T(1,128)} %broadcast_in_dim.90), calls=%async_computation | async-start | bytes 32768 | tf_op jit(solution)/shard_map/all_to_all | solution.py:26
  112.3 13.0 %all-to-all-start.5 = ((bf16[32,8,221]{2,1,0:T(8,128)(2,1)}), bf16[32,8,221]{2,1,0:T(8,128)(2,1)S(1)}, u32[]{:S(2)}, u32[]{:S(2)}) async-start(bf16[32,8,221]{2,1,0:T(8,128)(2,1)} %broadcast_in_dim.95), calls=%async_computation.5 | async-start | bytes 262144 | tf_op jit(solution)/shard_map/all_to_all | solution.py:26
  128.5 14.7 %all-to-all-start.6 = ((f32[32,1,128]{2,1,0:T(1,128)}), f32[32,1,128]{2,1,0:T(1,128)S(1)}, u32[]{:S(2)}, u32[]{:S(2)}) async-start(f32[32,1,128]{2,1,0:T(1,128)} %broadcast_in_dim.96), calls=%async_computation.6 | async-start | bytes 32768 | tf_op jit(solution)/shard_map/all_to_all | solution.py:26
  135.3 21.0 %collective-permute-start.10 = (bf16[1,300,128]{2,1,0:T(8,128)(2,1)}, bf16[1,300,128]{2,1,0:T(8,128)(2,1)S(1)}, u32[]{:S(2)}, u32[]{:S(2)}) collective-permute-start(bf16[1,300,128]{2,1,0:T(8,128)(2,1)} %get-tuple-element.48), channel_id=1, source_target_pairs={{32,0},{64,32},{96,64},{128,96},{160,128},{192,160},{224,192},{33,... | collective-permute-start | bytes 230408 | tf_op jit(solution)/shard_map/ppermute | solution.py:19
  138.4 22.0 %collective-permute-start.9 = (bf16[1,300,128]{2,1,0:T(8,128)(2,1)S(1)}, bf16[1,300,128]{2,1,0:T(8,128)(2,1)S(1)}, u32[]{:S(2)}, u32[]{:S(2)}) collective-permute-start(bf16[1,300,128]{2,1,0:T(8,128)(2,1)S(1)} %get-tuple-element.49), channel_id=1, source_target_pairs={{0,32},{32,64},{64,96},{96,128},{128,160},{160,192},{192,224},{1,3... | collective-permute-start | bytes 230408 | tf_op jit(solution)/shard_map/ppermute | solution.py:18
  143.8 12.4 %all-to-all-start.7 = ((f32[8,1,128]{2,1,0:T(1,128)}), f32[8,1,128]{2,1,0:T(1,128)S(1)}, u32[]{:S(2)}, u32[]{:S(2)}) async-start(f32[8,1,128]{2,1,0:T(1,128)} %broadcast_in_dim.97), calls=%async_computation.7 | async-start | bytes 8192 | tf_op jit(solution)/shard_map/all_to_all | solution.py:26
  227.8 13.0 %all-to-all-start.13 = ((bf16[32,8,221]{2,1,0:T(8,128)(2,1)}), bf16[32,8,221]{2,1,0:T(8,128)(2,1)S(1)}, u32[]{:S(2)}, u32[]{:S(2)}) async-start(bf16[32,8,221]{2,1,0:T(8,128)(2,1)} %broadcast_in_dim.101), calls=%async_computation.13 | async-start | bytes 262144 | tf_op jit(solution)/shard_map/all_to_all | solution.py:26
  246.3 14.7 %all-to-all-start.14 = ((f32[32,1,128]{2,1,0:T(1,128)}), f32[32,1,128]{2,1,0:T(1,128)S(1)}, u32[]{:S(2)}, u32[]{:S(2)}) async-start(f32[32,1,128]{2,1,0:T(1,128)} %broadcast_in_dim.102), calls=%async_computation.14 | async-start | bytes 32768 | tf_op jit(solution)/shard_map/all_to_all | solution.py:26
  254.2 23.1 %collective-permute-start.16 = (bf16[1,300,128]{2,1,0:T(8,128)(2,1)}, bf16[1,300,128]{2,1,0:T(8,128)(2,1)}, u32[]{:S(2)}, u32[]{:S(2)}) collective-permute-start(bf16[1,300,128]{2,1,0:T(8,128)(2,1)} %get-tuple-element.39), channel_id=1, source_target_pairs={{32,0},{64,32},{96,64},{128,96},{160,128},{192,160},{224,192},{33,... | collective-permute-start | bytes 230408 | tf_op jit(solution)/shard_map/ppermute | solution.py:19
  257.4 23.9 %collective-permute-start.15 = (bf16[1,300,128]{2,1,0:T(8,128)(2,1)}, bf16[1,300,128]{2,1,0:T(8,128)(2,1)}, u32[]{:S(2)}, u32[]{:S(2)}) collective-permute-start(bf16[1,300,128]{2,1,0:T(8,128)(2,1)} %get-tuple-element.40), channel_id=1, source_target_pairs={{0,32},{32,64},{64,96},{96,128},{128,160},{160,192},{192,224},{1,3... | collective-permute-start | bytes 230408 | tf_op jit(solution)/shard_map/ppermute | solution.py:18
  261.6 15.6 %all-to-all-start.15 = ((f32[8,1,128]{2,1,0:T(1,128)}), f32[8,1,128]{2,1,0:T(1,128)S(1)}, u32[]{:S(2)}, u32[]{:S(2)}) async-start(f32[8,1,128]{2,1,0:T(1,128)} %broadcast_in_dim.103), calls=%async_computation.15 | async-start | bytes 8192 | tf_op jit(solution)/shard_map/all_to_all | solution.py:26
  269.0 13.3 %collective-permute-start.18 = (bf16[1,300,128]{2,1,0:T(8,128)(2,1)}, bf16[1,300,128]{2,1,0:T(8,128)(2,1)}, u32[]{:S(2)}, u32[]{:S(2)}) collective-permute-start(bf16[1,300,128]{2,1,0:T(8,128)(2,1)} %get-tuple-element.37), channel_id=1, source_target_pairs={{8,0},{16,8},{24,16},{9,1},{17,9},{25,17},{10,2},{18,10},{26,18},{... | collective-permute-start | bytes 230408 | tf_op jit(solution)/shard_map/ppermute | solution.py:19
  270.3 12.0 %collective-permute-start.17 = (bf16[1,300,128]{2,1,0:T(8,128)(2,1)}, bf16[1,300,128]{2,1,0:T(8,128)(2,1)}, u32[]{:S(2)}, u32[]{:S(2)}) collective-permute-start(bf16[1,300,128]{2,1,0:T(8,128)(2,1)} %get-tuple-element.38), channel_id=1, source_target_pairs={{0,8},{8,16},{16,24},{1,9},{9,17},{17,25},{2,10},{10,18},{18,26},{... | collective-permute-start | bytes 230408 | tf_op jit(solution)/shard_map/ppermute | solution.py:18
  348.9 13.0 %all-to-all-start.21 = ((bf16[32,8,221]{2,1,0:T(8,128)(2,1)}), bf16[32,8,221]{2,1,0:T(8,128)(2,1)S(1)}, u32[]{:S(2)}, u32[]{:S(2)}) async-start(bf16[32,8,221]{2,1,0:T(8,128)(2,1)} %broadcast_in_dim.107), calls=%async_computation.21 | async-start | bytes 262144 | tf_op jit(solution)/shard_map/all_to_all | solution.py:26
  365.0 14.7 %all-to-all-start.22 = ((f32[32,1,128]{2,1,0:T(1,128)}), f32[32,1,128]{2,1,0:T(1,128)S(1)}, u32[]{:S(2)}, u32[]{:S(2)}) async-start(f32[32,1,128]{2,1,0:T(1,128)} %broadcast_in_dim.108), calls=%async_computation.22 | async-start | bytes 32768 | tf_op jit(solution)/shard_map/all_to_all | solution.py:26
  371.2 21.6 %collective-permute-start.22 = (bf16[1,300,128]{2,1,0:T(8,128)(2,1)S(1)}, bf16[1,300,128]{2,1,0:T(8,128)(2,1)S(1)}, u32[]{:S(2)}, u32[]{:S(2)}) collective-permute-start(bf16[1,300,128]{2,1,0:T(8,128)(2,1)S(1)} %get-tuple-element.30), channel_id=1, source_target_pairs={{32,0},{64,32},{96,64},{128,96},{160,128},{192,160},{224,192},{33,... | collective-permute-start | bytes 230408 | tf_op jit(solution)/shard_map/ppermute | solution.py:19
  374.4 22.4 %collective-permute-start.21 = (bf16[1,300,128]{2,1,0:T(8,128)(2,1)S(1)}, bf16[1,300,128]{2,1,0:T(8,128)(2,1)S(1)}, u32[]{:S(2)}, u32[]{:S(2)}) collective-permute-start(bf16[1,300,128]{2,1,0:T(8,128)(2,1)S(1)} %get-tuple-element.31), channel_id=1, source_target_pairs={{0,32},{32,64},{64,96},{96,128},{128,160},{160,192},{192,224},{1,3... | collective-permute-start | bytes 230408 | tf_op jit(solution)/shard_map/ppermute | solution.py:18
  380.3 12.4 %all-to-all-start.23 = ((f32[8,1,128]{2,1,0:T(1,128)}), f32[8,1,128]{2,1,0:T(1,128)S(1)}, u32[]{:S(2)}, u32[]{:S(2)}) async-start(f32[8,1,128]{2,1,0:T(1,128)} %broadcast_in_dim.109), calls=%async_computation.23 | async-start | bytes 8192 | tf_op jit(solution)/shard_map/all_to_all | solution.py:26
  (40 other events, 396.1 us)
where the time goes:
time: 405 us; the launch traced here: 402 us
  starting transfers between devices  140 us (35%)
  blocking collectives  133 us (33%)
  waiting for transfers between devices  47.3 us (12%)
  local copies, waits for them, and re-layouts  36.8 us (9%)
  matrix products  29.4 us (7%)
  other arithmetic  12.8 us (3%)
    all_to_all x6, blocking collectives, from_everyone(): return lax.all_to_all(copies, axis, split_axis=0, concat_axis=0, tiled=True)  71.7 us
    all_to_all x12, starting transfers between devices, from_everyone(): return lax.all_to_all(copies, axis, split_axis=0, concat_axis=0, tiled=True)  59.5 us
    ppermute x15, starting transfers between devices, with_halo(): before = lax.ppermute(last, axis, up)  52.6 us
    all_to_all x3, blocking collectives, sum_at_owner(): lax.all_to_all(pieces, axis, split_axis=0, concat_axis=0, tiled=True)  43.2 us
    all_to_all x12, waiting for transfers between devices, from_everyone(): return lax.all_to_all(copies, axis, split_axis=0, concat_axis=0, tiled=True)  33.6 us
    ppermute x12, starting transfers between devices, with_halo(): after = lax.ppermute(first, axis, down)  21.7 us
    all_to_all x2, blocking collectives, summed_rows(): lax.all_to_all(nearer.astype(jnp.bfloat16), far, split_axis=0, concat_axi...  18.2 us
    dot_general x3, matrix products, body(): jnp.dot(flex, signed, preferred_element_type=jnp.float32)  18 us
  transfers between devices with their start and end apart: 40, of which 15 were waited for; matrix products, arithmetic and copies ran while one was open for 9% of the time, Pallas kernels for 0%

commit v1 on v0

v1 whole, which is shorter than its diff:
```python
import jax
import jax.numpy as jnp
import numpy as np
from jax import lax
from jax.sharding import Mesh
from jax.sharding import PartitionSpec as P

ITERS = 3
GX = ("gx_0", "gx_1")
PLANE = ("gx_0", "gx_1", "gy")
BF16 = jnp.bfloat16
F32 = jnp.float32
MSG_ROWS = 32


def shifted(value, axis, up):
    size = lax.axis_size(axis)
    pairs = [(i, i + 1) for i in range(size - 1)]
    return lax.ppermute(value, axis, pairs if up else [(j, i) for i, j in pairs])


def from_everyone(value, axes):
    copies = jnp.broadcast_to(value, (lax.axis_size(axes), *value.shape))
    return lax.all_to_all(copies, axes, split_axis=0, concat_axis=0, tiled=True)


def split_pair(value):
    high = value.astype(BF16)
    low = (value - high.astype(F32)).astype(BF16)
    return high, low


def plane_sum_matrix(sx, sy, plane_rows):
    matrix = np.zeros((plane_rows, sx * sy * MSG_ROWS), np.float32)
    inner = (sx - 1) * (sy - 1) * 6
    for i in range(sx):
        for j in range(sy):
            base = (i * sy + j) * MSG_ROWS
            for kx in range(2):
                for ky in range(2):
                    a, b = i + kx, j + ky
                    if 1 <= a <= sx - 1 and 1 <= b <= sy - 1:
                        for kz in range(2):
                            for d in range(3):
                                row = (((a - 1) * (sy - 1) + b - 1) * 2 + kz) * 3 + d
                                matrix[row, base + 3 * (4 * kx + 2 * ky + kz) + d] = 1
            for n in range(3):
                matrix[inner + n, base + 24 + n] = 1
                matrix[inner + n, base + 27 + n] = 1
            matrix[inner + 3, base + 30] = 1
    return matrix


def line_sum_matrix(sx, sy, sz, plane_rows, coarse_rows, total_rows):
    matrix = np.zeros((total_rows, sz * plane_rows), np.float32)
    inner = (sx - 1) * (sy - 1) * 6
    for layer in range(sz):
        base = layer * plane_rows
        for point in range((sx - 1) * (sy - 1)):
            for kz in range(2):
                c = layer + kz
                if 1 <= c <= sz - 1:
                    for d in range(3):
                        row = 3 * (point * (sz - 1) + c - 1) + d
                        matrix[row, base + (point * 2 + kz) * 3 + d] = 1
        for n in range(3):
            matrix[coarse_rows + n, base + inner + n] = 1
            matrix[coarse_rows + n, base + inner + 3 + n] = 1
    return matrix


def body(dual_rhs, local_flex, corner_coupling, face_stiffness, coarse_inverse, corner_ids):
    owned_rhs = dual_rhs[0, 0, 0]
    flex = local_flex[0, 0, 0]
    coupling = corner_coupling[0, 0, 0]
    stiffness = face_stiffness[0, 0, 0]
    corner_list = corner_ids[0, 0, 0]
    faces, width, columns = (stiffness.shape[0], stiffness.shape[1], owned_rhs.shape[2])
    coarse_rows = coarse_inverse.shape[0]
    sx, sy, sz = (lax.axis_size(GX), lax.axis_size("gy"), lax.axis_size("gz"))
    axes = (GX, "gy", "gz")
    px, py, pz = (lax.axis_index(GX), lax.axis_index("gy"), lax.axis_index("gz"))
    sign = jnp.array([-1.0, 1.0, -1.0, 1.0, -1.0, 1.0], F32)[:, None, None]
    mask = jnp.stack(
        [px > 0, px < sx - 1, py > 0, py < sy - 1, pz > 0, pz < sz - 1]
    ).astype(F32)[:, None, None]

    inner_rows = (sx - 1) * (sy - 1) * 6
    plane_rows = -(-(inner_rows + 7) // 8) * 8
    total_rows = -(-(coarse_rows + 3) // 8) * 8
    plane_sum = jnp.asarray(plane_sum_matrix(sx, sy, plane_rows), BF16)
    line_sum = jnp.asarray(
        line_sum_matrix(sx, sy, sz, plane_rows, coarse_rows, total_rows), BF16
    )

    coupling_faces = coupling.reshape(24, faces, width)
    beyond, far_coupling, far_rhs = [None] * 6, [None] * 6, [None] * 3
    rhs_low = owned_rhs.astype(BF16)
    for a, axis in enumerate(axes):
        up = jnp.concatenate(
            [stiffness[2 * a + 1], coupling_faces[:, 2 * a + 1].T, rhs_low[a]], axis=1
        )
        down = jnp.concatenate([stiffness[2 * a], coupling_faces[:, 2 * a].T], axis=1)
        before = shifted(up, axis, True)
        after = shifted(down, axis, False)
        beyond[2 * a], beyond[2 * a + 1] = before[:, :width], after[:, :width]
        far_coupling[2 * a] = before[:, width : width + 24]
        far_coupling[2 * a + 1] = after[:, width:]
        far_rhs[a] = before[:, width + 24 :].astype(F32)
    beyond = jnp.stack(beyond)
    signed_own = jnp.stack([coupling_faces[:, f].T for f in range(6)])
    spread = jnp.concatenate([signed_own, -jnp.stack(far_coupling)], axis=2)
    spread = (spread * (sign * mask).astype(BF16)).astype(BF16)
    spread = jnp.concatenate([spread, spread], axis=2)

    moves = np.array(
        [[0, 0, 0], [-1, 0, 0], [1, 0, 0], [0, -1, 0], [0, 1, 0], [0, 0, -1], [0, 0, 1]]
    )
    corner = np.arange(8)
    offsets = np.stack([corner // 4, corner // 2 % 2, corner % 2], axis=1)
    points = np.repeat((moves[:, None, :] + offsets[None, :, :]).reshape(-1, 3), 3, axis=0)
    qx, qy, qz = (px + points[:, 0], py + points[:, 1], pz + points[:, 2])
    inside = (qx > 0) & (qx < sx) & (qy > 0) & (qy < sy) & (qz > 0) & (qz < sz)
    lattice = ((qx - 1) * (sy - 1) + (qy - 1)) * (sz - 1) + (qz - 1)
    used = jnp.where(inside, 3 * lattice + np.tile(np.arange(3), 56), -1)
    select = (used[:, None] == jnp.arange(coarse_rows)[None, :]).astype(BF16)

    def precondition(dual):
        low = dual.astype(BF16)
        own = jnp.einsum("fij,fjr->fir", stiffness, low, preferred_element_type=F32)
        far = jnp.einsum("fij,fjr->fir", beyond, low, preferred_element_type=F32)
        return 0.25 * mask * (own + far)

    def exchange(corner_part, inner, number_row):
        highs, lows = zip(*[split_pair(v) for v in inner])
        message = jnp.concatenate(
            [corner_part.astype(BF16), jnp.stack(highs), jnp.stack(lows), number_row]
        )
        plane = from_everyone(message, PLANE).reshape(-1, columns)
        plane = jnp.dot(plane_sum, plane, preferred_element_type=F32)
        highs, lows = split_pair(plane[inner_rows : inner_rows + 3])
        numbers = plane[inner_rows + 3 : inner_rows + 4].astype(BF16)
        spare = jnp.zeros((plane_rows - inner_rows - 7, columns), BF16)
        message = jnp.concatenate([plane[:inner_rows].astype(BF16), highs, lows, numbers, spare])
        line = from_everyone(message, "gz")
        total = jnp.dot(line_sum, line.reshape(-1, columns), preferred_element_type=F32)
        return total[:coarse_rows], total[coarse_rows : coarse_rows + 3], line[:, inner_rows + 6]

    residual = jnp.stack(
        [far_rhs[0], owned_rhs[0], far_rhs[1], owned_rhs[1], far_rhs[2], owned_rhs[2]]
    ) * mask
    place = px * sy + py
    number_row = jnp.where(jnp.arange(columns) == place, corner_list[0], 0).astype(BF16)
    number_row = jnp.stack([number_row, jnp.zeros_like(number_row)])
    blank_row = jnp.zeros_like(number_row)
    zero = jnp.zeros((columns,), F32)

    for iteration in range(ITERS):
        last = iteration + 1 == ITERS
        precond = precondition(residual)
        signed = (sign * precond).astype(BF16).reshape(faces * width, columns)
        image = jnp.dot(flex, signed, preferred_element_type=F32)
        corner_part = jnp.dot(coupling, signed, preferred_element_type=F32)
        image_low = image.astype(BF16).reshape(faces, width, columns)
        far_image = [None] * 6
        for a, axis in enumerate(axes):
            far_image[2 * a + 1] = shifted(image_low[2 * a], axis, False)
            if not last:
                far_image[2 * a] = shifted(image_low[2 * a + 1], axis, True)
        rho = jnp.sum(residual[1::2] * precond[1::2], axis=(0, 1))
        wide = signed.astype(F32)
        own_energy = jnp.sum(wide * image, axis=0)
        cross_energy = jnp.sum(wide * image_old, axis=0) if iteration else zero
        coarse_rhs, inner, numbers = exchange(
            corner_part, (rho, own_energy, cross_energy), blank_row if iteration else number_row
        )
        rho, own_energy, cross_energy = inner[0], inner[1], inner[2]
        if iteration == 0:
            order = numbers[:, : sx * sy].astype(F32).reshape(sz, sx, sy)[1:, 1:, 1:]
            order = jnp.transpose(order, (1, 2, 0)).reshape(-1).astype(jnp.int32)
            dofs = (3 * order[:, None] + jnp.arange(3)[None, :]).reshape(-1)
            pick = (dofs[:, None] == jnp.arange(coarse_rows)[None, :]).astype(BF16)
            inverse = jnp.dot(pick, coarse_inverse, preferred_element_type=F32).astype(BF16)
            inverse = lax.dot_general(
                inverse, pick, (((1,), (1,)), ((), ())), preferred_element_type=F32
            ).astype(BF16)
            chosen = jnp.dot(select, inverse, preferred_element_type=F32).astype(BF16)
        coarse_low = coarse_rhs.astype(BF16)
        coarse_sol = jnp.dot(inverse, coarse_low, preferred_element_type=F32)
        corner_sol = jnp.dot(chosen, coarse_low, preferred_element_type=F32)
        high, low = split_pair(corner_sol)
        high, low = high.reshape(7, 24, columns), low.reshape(7, 24, columns)

        def moved_face(f):
            corners = jnp.concatenate([high[0], high[1 + f], low[0], low[1 + f]])
            return jnp.dot(spread[f], corners, preferred_element_type=F32)

        def jump(f):
            near, far = image_low[f].astype(F32), far_image[f].astype(F32)
            return sign[f] * mask[f] * (near - far) + moved_face(f)

        chosen_faces = range(1, 6, 2) if last else range(6)
        operated = jnp.stack([jump(f) for f in chosen_faces])
        plus = precond[1::2]
        if iteration == 0:
            direction, image_old, operated_old = plus, image, operated
            coarse_rhs_old, coarse_sol_old, energy = coarse_rhs, coarse_sol, own_energy
        else:
            ratio = rho / rho_old
            direction = plus + ratio * direction
            operated_old = operated + ratio * (operated_old[1::2] if last else operated_old)
            image_old = image + ratio * image_old
            coarse_rhs_old = coarse_rhs + ratio * coarse_rhs_old
            coarse_sol_old = coarse_sol + ratio * coarse_sol_old
            energy = own_energy + 2.0 * ratio * cross_energy + ratio * ratio * energy
        rho_old = rho
        curvature = energy + jnp.sum(coarse_rhs_old * coarse_sol_old, axis=0)
        step = rho / curvature
        multiplier = step * direction + (multiplier if iteration else 0.0)
        residual = (residual[1::2] if last else residual) - step * operated_old
    return (multiplier[None, None, None], residual[None, None, None])


def solution(mesh):
    torus = Mesh(
        mesh.devices.reshape(4, 2, mesh.shape["gy"], mesh.shape["gz"]), ("gx_0", "gx_1", "gy", "gz")
    )
    in_specs = (
        P(GX, "gy", "gz", None, None, None),
        P(GX, "gy", "gz", None, None),
        P(GX, "gy", "gz", None, None),
        P(GX, "gy", "gz", None, None, None),
        P(),
        P(GX, "gy", "gz", None),
    )
    out_specs = (P(GX, "gy", "gz", None, None, None), P(GX, "gy", "gz", None, None, None))
    return jax.shard_map(body, mesh=torus, in_specs=in_specs, out_specs=out_specs, check_vma=False)
```

time: 405 us -> 235 us (0.58)
  blocking collectives: 133 us -> 32.7 us
  starting transfers between devices: 140 us -> 84.8 us
  waiting for transfers between devices: 47.3 us -> 12.5 us
  matrix products: 29.4 us -> 55.3 us
  local copies, waits for them, and re-layouts: 36.8 us -> 31 us
    all_to_all x11 -> x2, blocking collectives: 133 us -> 32.7 us  [from_everyone(): return lax.all_to_all(copies, axes, split_axis=0, concat_axis=0, tiled=True)]
    all_to_all x13 -> x4, starting transfers between devices: 66 us -> 32.7 us  [from_everyone(): return lax.all_to_all(copies, axes, split_axis=0, concat_axis=0, tiled=True)]
    all_to_all x13 -> x4, waiting for transfers between devices: 37.1 us -> 5.63 us  [from_everyone(): return lax.all_to_all(copies, axes, split_axis=0, concat_axis=0, tiled=True)]
    dot_general x24 -> x41, matrix products: 29.4 us -> 55.3 us  [the longest x15 20.7 us: moved_face(): return jnp.dot(spread[f], corners, preferred_element_type=F32)]
    ppermute x27 -> x21, starting transfers between devices: 74.3 us -> 52 us  [shifted(): lax.ppermute(value, axis, pairs if up else [(j, i) for i, j in pairs])]
    convert_element_type x12 -> x22, other arithmetic: 6.89 us -> 0.74 us  [the longest x1 0.6 us: body(): spread = (spread * (sign * mask).astype(BF16)).astype(BF16)]
    broadcast_in_dim x19 -> x7, local copies, waits for them, and re-layouts: 7.59 us -> 3.06 us  [the longest x6 3.05 us: from_everyone(): copies = jnp.broadcast_to(value, (lax.axis_size(axes), *value.shape))]
    concatenate x0 -> x6, other arithmetic: none -> 4.34 us  [the longest x3 2.65 us: body(): jnp.concatenate([stiffness[2 * a + 1], coupling_faces[:, 2 * a + 1].T, rh...]
  transfers between devices with their start and end apart: 40 -> 25, of which waited for: 15 -> 4; matrix products, arithmetic and copies ran while one was open for 9% -> 20% of each run, Pallas kernels for 0% -> 0%
where the time goes in v1:
time: 235 us; the launch traced here: 233 us
  starting transfers between devices  84.8 us (36%)
  matrix products  55.3 us (24%)
  blocking collectives  32.7 us (14%)
  local copies, waits for them, and re-layouts  31 us (13%)
  waiting for transfers between devices  12.5 us (5%)
  other arithmetic  12.4 us (5%)
  between operations  4.16 us (2%)
    ppermute x21, starting transfers between devices, shifted(): lax.ppermute(value, axis, pairs if up else [(j, i) for i, j in pairs])  52 us
    all_to_all x4, starting transfers between devices, from_everyone(): return lax.all_to_all(copies, axes, split_axis=0, concat_axis=0, tiled=True)  32.7 us
    all_to_all x2, blocking collectives, from_everyone(): return lax.all_to_all(copies, axes, split_axis=0, concat_axis=0, tiled=True)  32.7 us
    dot_general x15, matrix products, moved_face(): return jnp.dot(spread[f], corners, preferred_element_type=F32)  20.7 us
    dot_general x3, matrix products, body(): image = jnp.dot(flex, signed, preferred_element_type=F32)  18.6 us
    unnamed x180, local copies, waits for them, and re-layouts  12.1 us
    ppermute x21, waiting for transfers between devices, shifted(): lax.ppermute(value, axis, pairs if up else [(j, i) for i, j in pairs])  6.86 us
    all_to_all x4, waiting for transfers between devices, from_everyone(): return lax.all_to_all(copies, axes, split_axis=0, concat_axis=0, tiled=True)  5.63 us
  transfers between devices with their start and end apart: 25, of which 4 were waited for; matrix products, arithmetic and copies ran while one was open for 20% of the time, Pallas kernels for 0%

profile of v1, /device:TPU:1, one launch (start us, length us, event | category | flops | bytes accessed | tf_op | source)
XLA Modules:
  0.0 232.7 jit_solution(9773499176683773514)
XLA Ops:
  4.7 4.5 %collective-permute-start = (bf16[300,452]{1,0:T(8,128)(2,1)}, bf16[300,452]{1,0:T(8,128)(2,1)S(1)}, u32[]{:S(2)}, u32[]{:S(2)}) collective-permute-start(bf16[300,452]{1,0:T(8,128)(2,1)} %pad_maximum_fusion), channel_id=1, source_target_pairs={{0,32},{32,64},{64,96},{96,128},{128,160},{160,192},{192,224},{1,3... | collective-permute-start | bytes 813608 | tf_op jit(solution)/shard_map/ppermute | solution.py:19
  10.2 3.2 %collective-permute-start.1 = (bf16[300,452]{1,0:T(8,128)(2,1)}, bf16[300,452]{1,0:T(8,128)(2,1)S(1)}, u32[]{:S(2)}, u32[]{:S(2)}) collective-permute-start(bf16[300,452]{1,0:T(8,128)(2,1)} %pad_maximum_fusion.1), channel_id=1, source_target_pairs={{0,8},{8,16},{16,24},{1,9},{9,17},{17,25},{2,10},{10,18},{18,26},{... | collective-permute-start | bytes 813608 | tf_op jit(solution)/shard_map/ppermute | solution.py:19
  14.4 4.3 %collective-permute-start.2 = (bf16[300,452]{1,0:T(8,128)(2,1)}, bf16[300,452]{1,0:T(8,128)(2,1)}, u32[]{:S(2)}, u32[]{:S(2)}) collective-permute-start(bf16[300,452]{1,0:T(8,128)(2,1)} %pad_maximum_fusion.2), channel_id=1, source_target_pairs={{0,1},{1,2},{2,3},{3,4},{4,5},{5,6},{6,7},{8,9},{9,10},{10,11},{11... | collective-permute-start | bytes 813608 | tf_op jit(solution)/shard_map/ppermute | solution.py:19
  31.5 5.7 %collective-permute-done.5 = bf16[300,324]{1,0:T(8,128)(2,1)S(1)} collective-permute-done((bf16[300,324]{1,0:T(8,128)(2,1)S(1)}, bf16[300,324]{1,0:T(8,128)(2,1)S(1)}, u32[]{:S(2)}, u32[]{:S(2)}) %collective-permute-start.5) | collective-permute-done | bytes 194432 | tf_op jit(solution)/shard_map/ppermute | solution.py:19
  44.6 6.0 %multiply_reduce_fusion = (f32[128]{0:T(128)S(1)}, bf16[1800,128]{1,0:T(8,128)(2,1)S(1)}, f32[1800,128]{1,0:T(8,128)}) fusion(bf16[1800,128]{1,0:T(8,128)(2,1)S(1)} %reshape.616, bf16[1,1,1,1800,1800]{4,3,2,1,0:T(8,128)(2,1)} %param.14), kind=kOutput, calls=%fused_computation.51 | convolution fusion | flops 830361472 | bytes 8323712 | tf_op jit(solution)/shard_map/dot_general | solution.py:162
  51.7 9.1 %all-to-all-start = ((bf16[32,32,128]{2,1,0:T(8,128)(2,1)}), bf16[32,32,128]{2,1,0:T(8,128)(2,1)S(1)}, u32[]{:S(2)}, u32[]{:S(2)}) async-start(bf16[32,32,128]{2,1,0:T(8,128)(2,1)} %broadcast_in_dim.30), calls=%async_computation | async-start | bytes 524288 | tf_op jit(solution)/shard_map/all_to_all | solution.py:24
  61.6 3.7 %collective-permute-start.6 = (bf16[300,128]{1,0:T(8,128)(2,1)}, bf16[300,128]{1,0:T(8,128)(2,1)}, u32[]{:S(2)}, u32[]{:S(2)}) collective-permute-start(bf16[300,128]{1,0:T(8,128)(2,1)} %get-tuple-element.56), channel_id=1, source_target_pairs={{0,32},{32,64},{64,96},{96,128},{128,160},{160,192},{192,224},{1,3... | collective-permute-start | bytes 230408 | tf_op jit(solution)/shard_map/ppermute | solution.py:19
  70.8 7.3 %all-to-all-start.1 = ((bf16[8,136,128]{2,1,0:T(8,128)(2,1)}), bf16[8,136,128]{2,1,0:T(8,128)(2,1)S(1)}, u32[]{:S(2)}, u32[]{:S(2)}) async-start(bf16[8,136,128]{2,1,0:T(8,128)(2,1)} %broadcast_in_dim.31), calls=%async_computation.1 | async-start | bytes 557056 | tf_op jit(solution)/shard_map/all_to_all | solution.py:24
  80.2 2.8 %collective-permute-start.7 = (bf16[300,128]{1,0:T(8,128)(2,1)}, bf16[300,128]{1,0:T(8,128)(2,1)}, u32[]{:S(2)}, u32[]{:S(2)}) collective-permute-start(bf16[300,128]{1,0:T(8,128)(2,1)} %get-tuple-element.57), channel_id=1, source_target_pairs={{32,0},{64,32},{96,64},{128,96},{160,128},{192,160},{224,192},{33,... | collective-permute-start | bytes 230408 | tf_op jit(solution)/shard_map/ppermute | solution.py:19
  83.0 2.2 collective-permute-start.8
  86.4 4.3 %collective-permute-start.10 = (bf16[300,128]{1,0:T(8,128)(2,1)}, bf16[300,128]{1,0:T(8,128)(2,1)}, u32[]{:S(2)}, u32[]{:S(2)}) collective-permute-start(bf16[300,128]{1,0:T(8,128)(2,1)} %get-tuple-element.53), channel_id=1, source_target_pairs={{0,1},{1,2},{2,3},{3,4},{4,5},{5,6},{6,7},{8,9},{9,10},{10,11},{11... | collective-permute-start | bytes 230408 | tf_op jit(solution)/shard_map/ppermute | solution.py:19
  110.3 6.4 %fusion.39 = (f32[128]{0:T(128)S(1)}, f32[128]{0:T(128)S(1)}, bf16[1800,128]{1,0:T(8,128)(2,1)}, f32[1800,128]{1,0:T(8,128)}) fusion(f32[1800,128]{1,0:T(8,128)} %get-tuple-element.109, bf16[1800,128]{1,0:T(8,128)(2,1)S(1)} %reshape.620, bf16[1,1,1,1800,1800]{4,3,2,1,0:T(8,128)(2,1)} %param.14), kind=kOutput, calls=%fused_computation.48 | convolution fusion | flops 830822144 | bytes 9245824 | tf_op jit(solution)/shard_map/dot_general | solution.py:162
  117.2 16.1 %all_to_all.30 = bf16[32,32,128]{2,1,0:T(8,128)(2,1)S(1)} all-to-all(bf16[32,32,128]{2,1,0:T(8,128)(2,1)S(1)} %broadcast_in_dim.33), channel_id=1, replica_groups=mesh['gx_0'=4,'gx_1'=2,'gy'=4,'gz'=8] {'gx_0','gx_1','gy'}, dimensions={0} | all-to-all | bytes 524288 | tf_op jit(solution)/shard_map/all_to_all | solution.py:24
  135.4 8.1 %all-to-all-start.3 = ((bf16[8,136,128]{2,1,0:T(8,128)(2,1)}), bf16[8,136,128]{2,1,0:T(8,128)(2,1)}, u32[]{:S(2)}, u32[]{:S(2)}) async-start(bf16[8,136,128]{2,1,0:T(8,128)(2,1)} %broadcast_in_dim.34), calls=%async_computation.3 | async-start | bytes 557056 | tf_op jit(solution)/shard_map/all_to_all | solution.py:24
  143.5 1.9 fusion.234
  145.5 2.9 %collective-permute-start.12 = (bf16[300,128]{1,0:T(8,128)(2,1)}, bf16[300,128]{1,0:T(8,128)(2,1)}, u32[]{:S(2)}, u32[]{:S(2)}) collective-permute-start(bf16[300,128]{1,0:T(8,128)(2,1)} %get-tuple-element.50), channel_id=1, source_target_pairs={{0,32},{32,64},{64,96},{96,128},{128,160},{160,192},{192,224},{1,3... | collective-permute-start | bytes 230408 | tf_op jit(solution)/shard_map/ppermute | solution.py:19
  148.4 2.0 collective-permute-start.13
  150.4 2.9 %collective-permute-start.14 = (bf16[300,128]{1,0:T(8,128)(2,1)}, bf16[300,128]{1,0:T(8,128)(2,1)}, u32[]{:S(2)}, u32[]{:S(2)}) collective-permute-start(bf16[300,128]{1,0:T(8,128)(2,1)} %get-tuple-element.48), channel_id=1, source_target_pairs={{0,8},{8,16},{16,24},{1,9},{9,17},{17,25},{2,10},{10,18},{18,26},{... | collective-permute-start | bytes 230408 | tf_op jit(solution)/shard_map/ppermute | solution.py:19
  154.6 4.0 %collective-permute-start.16 = (bf16[300,128]{1,0:T(8,128)(2,1)}, bf16[300,128]{1,0:T(8,128)(2,1)}, u32[]{:S(2)}, u32[]{:S(2)}) collective-permute-start(bf16[300,128]{1,0:T(8,128)(2,1)} %get-tuple-element.47), channel_id=1, source_target_pairs={{0,1},{1,2},{2,3},{3,4},{4,5},{5,6},{6,7},{8,9},{9,10},{10,11},{11... | collective-permute-start | bytes 230408 | tf_op jit(solution)/shard_map/ppermute | solution.py:19
  177.6 6.1 %fusion.41 = (f32[128]{0:T(128)S(1)}, f32[128]{0:T(128)S(1)}, bf16[1800,128]{1,0:T(8,128)(2,1)}) fusion(bf16[1800,128]{1,0:T(8,128)(2,1)S(1)} %reshape.623, f32[1800,128]{1,0:T(8,128)} %get-tuple-element.116, f32[1800,128]{1,0:T(8,128)S(1)} %copy-done.9, f32[128]{0:T(128)S(1)} %copy-done.58, bf16[1,1,1,1800,1800]{4,3,2,1,0:T(8,128)(2,1)} %param.14), kind=kOutput, calls=%fused_computation.50 | convolution fusion | flops 831282944 | bytes 9246336 | tf_op jit(solution)/shard_map/dot_general | solution.py:162
  184.1 16.6 %all_to_all.31 = bf16[32,32,128]{2,1,0:T(8,128)(2,1)S(1)} all-to-all(bf16[32,32,128]{2,1,0:T(8,128)(2,1)S(1)} %broadcast_in_dim.35), channel_id=1, replica_groups=mesh['gx_0'=4,'gx_1'=2,'gy'=4,'gz'=8] {'gx_0','gx_1','gy'}, dimensions={0} | all-to-all | bytes 524288 | tf_op jit(solution)/shard_map/all_to_all | solution.py:24
  201.8 8.2 %all-to-all-start.5 = ((bf16[8,136,128]{2,1,0:T(8,128)(2,1)}), bf16[8,136,128]{2,1,0:T(8,128)(2,1)S(1)}, u32[]{:S(2)}, u32[]{:S(2)}) async-start(bf16[8,136,128]{2,1,0:T(8,128)(2,1)} %broadcast_in_dim.36), calls=%async_computation.5 | async-start | bytes 557056 | tf_op jit(solution)/shard_map/all_to_all | solution.py:24
  211.7 3.0 %collective-permute-start.18 = (bf16[300,128]{1,0:T(8,128)(2,1)}, bf16[300,128]{1,0:T(8,128)(2,1)}, u32[]{:S(2)}, u32[]{:S(2)}) collective-permute-start(bf16[300,128]{1,0:T(8,128)(2,1)} %get-tuple-element.43), channel_id=1, source_target_pairs={{32,0},{64,32},{96,64},{128,96},{160,128},{192,160},{224,192},{33,... | collective-permute-start | bytes 230408 | tf_op jit(solution)/shard_map/ppermute | solution.py:19
  217.3 3.7 %all-to-all-done.5 = bf16[8,136,128]{2,1,0:T(8,128)(2,1)S(1)} async-done(((bf16[8,136,128]{2,1,0:T(8,128)(2,1)}), bf16[8,136,128]{2,1,0:T(8,128)(2,1)S(1)}, u32[]{:S(2)}, u32[]{:S(2)}) %all-to-all-start.5) | async-done | bytes 278560 | tf_op jit(solution)/shard_map/all_to_all | solution.py:24
  (367 shorter events, 93.6 us)
Async XLA Ops:
  4.7 32.7 %collective-permute-start = (bf16[300,452]{1,0:T(8,128)(2,1)}, bf16[300,452]{1,0:T(8,128)(2,1)S(1)}, u32[]{:S(2)}, u32[]{:S(2)}) collective-permute-start(bf16[300,452]{1,0:T(8,128)(2,1)} %pad_maximum_fusion), channel_id=1, source_target_pairs={{0,32},{32,64},{64,96},{96,128},{128,160},{160,192},{192,224},{1,3... | collective-permute-start | bytes 813608 | tf_op jit(solution)/shard_map/ppermute | solution.py:19
  10.2 27.3 %collective-permute-start.1 = (bf16[300,452]{1,0:T(8,128)(2,1)}, bf16[300,452]{1,0:T(8,128)(2,1)S(1)}, u32[]{:S(2)}, u32[]{:S(2)}) collective-permute-start(bf16[300,452]{1,0:T(8,128)(2,1)} %pad_maximum_fusion.1), channel_id=1, source_target_pairs={{0,8},{8,16},{16,24},{1,9},{9,17},{17,25},{2,10},{10,18},{18,26},{... | collective-permute-start | bytes 813608 | tf_op jit(solution)/shard_map/ppermute | solution.py:19
  14.4 23.2 %collective-permute-start.2 = (bf16[300,452]{1,0:T(8,128)(2,1)}, bf16[300,452]{1,0:T(8,128)(2,1)}, u32[]{:S(2)}, u32[]{:S(2)}) collective-permute-start(bf16[300,452]{1,0:T(8,128)(2,1)} %pad_maximum_fusion.2), channel_id=1, source_target_pairs={{0,1},{1,2},{2,3},{3,4},{4,5},{5,6},{6,7},{8,9},{9,10},{10,11},{11... | collective-permute-start | bytes 813608 | tf_op jit(solution)/shard_map/ppermute | solution.py:19
  19.7 9.0 %collective-permute-start.3 = (bf16[300,324]{1,0:T(8,128)(2,1)}, bf16[300,324]{1,0:T(8,128)(2,1)S(1)}, u32[]{:S(2)}, u32[]{:S(2)}) collective-permute-start(bf16[300,324]{1,0:T(8,128)(2,1)} %pad_maximum_fusion.3), channel_id=1, source_target_pairs={{32,0},{64,32},{96,64},{128,96},{160,128},{192,160},{224,192},{33,... | collective-permute-start | bytes 583208 | tf_op jit(solution)/shard_map/ppermute | solution.py:19
  22.6 8.7 %collective-permute-start.4 = (bf16[300,324]{1,0:T(8,128)(2,1)}, bf16[300,324]{1,0:T(8,128)(2,1)S(1)}, u32[]{:S(2)}, u32[]{:S(2)}) collective-permute-start(bf16[300,324]{1,0:T(8,128)(2,1)} %pad_maximum_fusion.4), channel_id=1, source_target_pairs={{8,0},{16,8},{24,16},{9,1},{17,9},{25,17},{10,2},{18,10},{26,18},{... | collective-permute-start | bytes 583208 | tf_op jit(solution)/shard_map/ppermute | solution.py:19
  28.7 8.5 %collective-permute-start.5 = (bf16[300,324]{1,0:T(8,128)(2,1)S(1)}, bf16[300,324]{1,0:T(8,128)(2,1)S(1)}, u32[]{:S(2)}, u32[]{:S(2)}) collective-permute-start(bf16[300,324]{1,0:T(8,128)(2,1)S(1)} %pad_maximum_fusion.5), channel_id=1, source_target_pairs={{1,0},{2,1},{3,2},{4,3},{5,4},{6,5},{7,6},{9,8},{10,9},{11,10},{12... | collective-permute-start | bytes 583208 | tf_op jit(solution)/shard_map/ppermute | solution.py:19
  51.7 17.9 %all-to-all-start = ((bf16[32,32,128]{2,1,0:T(8,128)(2,1)}), bf16[32,32,128]{2,1,0:T(8,128)(2,1)S(1)}, u32[]{:S(2)}, u32[]{:S(2)}) async-start(bf16[32,32,128]{2,1,0:T(8,128)(2,1)} %broadcast_in_dim.30), calls=%async_computation | async-start | bytes 524288 | tf_op jit(solution)/shard_map/all_to_all | solution.py:24
  61.6 33.9 %collective-permute-start.6 = (bf16[300,128]{1,0:T(8,128)(2,1)}, bf16[300,128]{1,0:T(8,128)(2,1)}, u32[]{:S(2)}, u32[]{:S(2)}) collective-permute-start(bf16[300,128]{1,0:T(8,128)(2,1)} %get-tuple-element.56), channel_id=1, source_target_pairs={{0,32},{32,64},{64,96},{96,128},{128,160},{160,192},{192,224},{1,3... | collective-permute-start | bytes 230408 | tf_op jit(solution)/shard_map/ppermute | solution.py:19
  70.8 20.1 %all-to-all-start.1 = ((bf16[8,136,128]{2,1,0:T(8,128)(2,1)}), bf16[8,136,128]{2,1,0:T(8,128)(2,1)S(1)}, u32[]{:S(2)}, u32[]{:S(2)}) async-start(bf16[8,136,128]{2,1,0:T(8,128)(2,1)} %broadcast_in_dim.31), calls=%async_computation.1 | async-start | bytes 557056 | tf_op jit(solution)/shard_map/all_to_all | solution.py:24
  80.2 18.0 %collective-permute-start.7 = (bf16[300,128]{1,0:T(8,128)(2,1)}, bf16[300,128]{1,0:T(8,128)(2,1)}, u32[]{:S(2)}, u32[]{:S(2)}) collective-permute-start(bf16[300,128]{1,0:T(8,128)(2,1)} %get-tuple-element.57), channel_id=1, source_target_pairs={{32,0},{64,32},{96,64},{128,96},{160,128},{192,160},{224,192},{33,... | collective-permute-start | bytes 230408 | tf_op jit(solution)/shard_map/ppermute | solution.py:19
  83.0 17.1 %collective-permute-start.8 = (bf16[300,128]{1,0:T(8,128)(2,1)}, bf16[300,128]{1,0:T(8,128)(2,1)}, u32[]{:S(2)}, u32[]{:S(2)}) collective-permute-start(bf16[300,128]{1,0:T(8,128)(2,1)} %get-tuple-element.54), channel_id=1, source_target_pairs={{0,8},{8,16},{16,24},{1,9},{9,17},{17,25},{2,10},{10,18},{18,26},{... | collective-permute-start | bytes 230408 | tf_op jit(solution)/shard_map/ppermute | solution.py:19
  85.1 16.0 %collective-permute-start.9 = (bf16[300,128]{1,0:T(8,128)(2,1)}, bf16[300,128]{1,0:T(8,128)(2,1)}, u32[]{:S(2)}, u32[]{:S(2)}) collective-permute-start(bf16[300,128]{1,0:T(8,128)(2,1)} %get-tuple-element.55), channel_id=1, source_target_pairs={{8,0},{16,8},{24,16},{9,1},{17,9},{25,17},{10,2},{18,10},{26,18},{... | collective-permute-start | bytes 230408 | tf_op jit(solution)/shard_map/ppermute | solution.py:19
  86.4 16.4 %collective-permute-start.10 = (bf16[300,128]{1,0:T(8,128)(2,1)}, bf16[300,128]{1,0:T(8,128)(2,1)}, u32[]{:S(2)}, u32[]{:S(2)}) collective-permute-start(bf16[300,128]{1,0:T(8,128)(2,1)} %get-tuple-element.53), channel_id=1, source_target_pairs={{0,1},{1,2},{2,3},{3,4},{4,5},{5,6},{6,7},{8,9},{9,10},{10,11},{11... | collective-permute-start | bytes 230408 | tf_op jit(solution)/shard_map/ppermute | solution.py:19
  135.4 23.2 %all-to-all-start.3 = ((bf16[8,136,128]{2,1,0:T(8,128)(2,1)}), bf16[8,136,128]{2,1,0:T(8,128)(2,1)}, u32[]{:S(2)}, u32[]{:S(2)}) async-start(bf16[8,136,128]{2,1,0:T(8,128)(2,1)} %broadcast_in_dim.34), calls=%async_computation.3 | async-start | bytes 557056 | tf_op jit(solution)/shard_map/all_to_all | solution.py:24
  145.5 16.3 %collective-permute-start.12 = (bf16[300,128]{1,0:T(8,128)(2,1)}, bf16[300,128]{1,0:T(8,128)(2,1)}, u32[]{:S(2)}, u32[]{:S(2)}) collective-permute-start(bf16[300,128]{1,0:T(8,128)(2,1)} %get-tuple-element.50), channel_id=1, source_target_pairs={{0,32},{32,64},{64,96},{96,128},{128,160},{160,192},{192,224},{1,3... | collective-permute-start | bytes 230408 | tf_op jit(solution)/shard_map/ppermute | solution.py:19
  148.4 15.8 %collective-permute-start.13 = (bf16[300,128]{1,0:T(8,128)(2,1)}, bf16[300,128]{1,0:T(8,128)(2,1)}, u32[]{:S(2)}, u32[]{:S(2)}) collective-permute-start(bf16[300,128]{1,0:T(8,128)(2,1)} %get-tuple-element.51), channel_id=1, source_target_pairs={{32,0},{64,32},{96,64},{128,96},{160,128},{192,160},{224,192},{33,... | collective-permute-start | bytes 230408 | tf_op jit(solution)/shard_map/ppermute | solution.py:19
  150.4 15.6 %collective-permute-start.14 = (bf16[300,128]{1,0:T(8,128)(2,1)}, bf16[300,128]{1,0:T(8,128)(2,1)}, u32[]{:S(2)}, u32[]{:S(2)}) collective-permute-start(bf16[300,128]{1,0:T(8,128)(2,1)} %get-tuple-element.48), channel_id=1, source_target_pairs={{0,8},{8,16},{16,24},{1,9},{9,17},{17,25},{2,10},{10,18},{18,26},{... | collective-permute-start | bytes 230408 | tf_op jit(solution)/shard_map/ppermute | solution.py:19
  153.3 13.8 %collective-permute-start.15 = (bf16[300,128]{1,0:T(8,128)(2,1)}, bf16[300,128]{1,0:T(8,128)(2,1)}, u32[]{:S(2)}, u32[]{:S(2)}) collective-permute-start(bf16[300,128]{1,0:T(8,128)(2,1)} %get-tuple-element.49), channel_id=1, source_target_pairs={{8,0},{16,8},{24,16},{9,1},{17,9},{25,17},{10,2},{18,10},{26,18},{... | collective-permute-start | bytes 230408 | tf_op jit(solution)/shard_map/ppermute | solution.py:19
  154.6 14.2 %collective-permute-start.16 = (bf16[300,128]{1,0:T(8,128)(2,1)}, bf16[300,128]{1,0:T(8,128)(2,1)}, u32[]{:S(2)}, u32[]{:S(2)}) collective-permute-start(bf16[300,128]{1,0:T(8,128)(2,1)} %get-tuple-element.47), channel_id=1, source_target_pairs={{0,1},{1,2},{2,3},{3,4},{4,5},{5,6},{6,7},{8,9},{9,10},{10,11},{11... | collective-permute-start | bytes 230408 | tf_op jit(solution)/shard_map/ppermute | solution.py:19
  161.7 8.8 %collective-permute-start.17 = (bf16[300,128]{1,0:T(8,128)(2,1)S(1)}, bf16[300,128]{1,0:T(8,128)(2,1)S(1)}, u32[]{:S(2)}, u32[]{:S(2)}) collective-permute-start(bf16[300,128]{1,0:T(8,128)(2,1)S(1)} %get-tuple-element.46), channel_id=1, source_target_pairs={{1,0},{2,1},{3,2},{4,3},{5,4},{6,5},{7,6},{9,8},{10,9},{11,10},{12... | collective-permute-start | bytes 230408 | tf_op jit(solution)/shard_map/ppermute | solution.py:19
  201.8 19.2 %all-to-all-start.5 = ((bf16[8,136,128]{2,1,0:T(8,128)(2,1)}), bf16[8,136,128]{2,1,0:T(8,128)(2,1)S(1)}, u32[]{:S(2)}, u32[]{:S(2)}) async-start(bf16[8,136,128]{2,1,0:T(8,128)(2,1)} %broadcast_in_dim.36), calls=%async_computation.5 | async-start | bytes 557056 | tf_op jit(solution)/shard_map/all_to_all | solution.py:24
  211.7 13.0 %collective-permute-start.18 = (bf16[300,128]{1,0:T(8,128)(2,1)}, bf16[300,128]{1,0:T(8,128)(2,1)}, u32[]{:S(2)}, u32[]{:S(2)}) collective-permute-start(bf16[300,128]{1,0:T(8,128)(2,1)} %get-tuple-element.43), channel_id=1, source_target_pairs={{32,0},{64,32},{96,64},{128,96},{160,128},{192,160},{224,192},{33,... | collective-permute-start | bytes 230408 | tf_op jit(solution)/shard_map/ppermute | solution.py:19
  214.7 11.8 %collective-permute-start.19 = (bf16[300,128]{1,0:T(8,128)(2,1)}, bf16[300,128]{1,0:T(8,128)(2,1)}, u32[]{:S(2)}, u32[]{:S(2)}) collective-permute-start(bf16[300,128]{1,0:T(8,128)(2,1)} %get-tuple-element.45), channel_id=1, source_target_pairs={{8,0},{16,8},{24,16},{9,1},{17,9},{25,17},{10,2},{18,10},{26,18},{... | collective-permute-start | bytes 230408 | tf_op jit(solution)/shard_map/ppermute | solution.py:19
  216.0 12.1 %collective-permute-start.20 = (bf16[300,128]{1,0:T(8,128)(2,1)S(1)}, bf16[300,128]{1,0:T(8,128)(2,1)}, u32[]{:S(2)}, u32[]{:S(2)}) collective-permute-start(bf16[300,128]{1,0:T(8,128)(2,1)S(1)} %get-tuple-element.44), channel_id=1, source_target_pairs={{1,0},{2,1},{3,2},{4,3},{5,4},{6,5},{7,6},{9,8},{10,9},{11,10},{12... | collective-permute-start | bytes 230408 | tf_op jit(solution)/shard_map/ppermute | solution.py:19
  (77 other events, 615.6 us)
